TPU v7x, 16 devices: a 4x2x1 block of a 4x4x8 slice. The times are simulated.
16 devices in a mesh: data: 2 (over y, z), tp: 8 (over x, core).
Axes of the slice: x: 4, y: 2, z: 1, core: 2. Of those that a mesh axis runs over, the one named last changes fastest.
The devices are a block of a 4x4x8 slice.
Arguments:
- x_in: bfloat16 [16384, 2048], P('data'), parts along dimension 0
- w_gate: bfloat16 [2048, 8192], P(None, 'tp')
- w_up: bfloat16 [2048, 8192], P(None, 'tp')
- w_down: bfloat16 [8192, 2048], P('tp')
- residual: bfloat16 [16384, 2048], P(('data', 'tp')), parts along dimension 0
- norm_gain: float32 [2048], replicated
Outputs:
- output 1: bfloat16 [16384, 2048], P(('data', 'tp')), parts along dimension 0
- output 2: bfloat16 [16384, 2048], P(('data', 'tp')), parts along dimension 0
There are 2 independent parts. A program takes and returns all parts, laid end to end along the dimension named above; an argument that names none is the same for every part.
All inputs are finite; a program needn't handle non-finite values.
Results may differ from a plain program's by a relative error of at most 0.00647883.
Values are sent between devices in bfloat16 or wider.
A program may use at most 768 MiB of HBM per device.

v0:
```python
import jax
import jax.numpy as jnp
from jax import lax
from jax.sharding import PartitionSpec as P

EPS = 1e-5


def add_and_norm(y_sum, residual, norm_gain):
    hidden_sum = residual.astype(jnp.float32) + y_sum
    mean_sq = jnp.mean(hidden_sum * hidden_sum, axis=-1, keepdims=True)
    normed = hidden_sum * lax.rsqrt(mean_sq + EPS) * norm_gain
    return hidden_sum.astype(jnp.bfloat16), normed.astype(jnp.bfloat16)


def solution(mesh):
    tp_size = mesh.shape["tp"]

    def local_block(x_in, w_gate, w_up, w_down, residual, norm_gain):
        gate_val = jnp.dot(x_in, w_gate, preferred_element_type=jnp.float32)
        up_val = jnp.dot(x_in, w_up, preferred_element_type=jnp.float32)
        hidden = (jax.nn.silu(gate_val) * up_val).astype(jnp.bfloat16)
        part_prod = jnp.dot(hidden, w_down, preferred_element_type=jnp.float32).astype(jnp.bfloat16)
        received = lax.all_to_all(part_prod, "tp", 0, 0, tiled=True)
        rows = residual.shape[0]
        y_sum = jnp.sum(received.reshape(tp_size, rows, received.shape[1]), axis=0, dtype=jnp.float32)
        return add_and_norm(y_sum, residual, norm_gain)

    row_spec = P(("data", "tp"), None)
    return jax.shard_map(local_block, mesh=mesh, in_specs=(P("data", None), P(None, "tp"), P(None, "tp"), P("tp", None), row_spec, P(None)), out_specs=(row_spec, row_spec), check_vma=False)
```

profile of v0, /device:TPU:112, one launch (start us, length us, event | category | flops | bytes accessed | tf_op | source)
XLA Modules:
  0.0 540.6 jit_solution(10485412511149074281)
XLA Ops:
  0.6 42.3 %fusion.1 = f32[8192,1024]{1,0:T(8,128)} fusion(bf16[8192,2048]{1,0:T(8,128)(2,1)} %param.6, bf16[2048,1024]{1,0:T(8,128)(2,1)} %param.7), kind=kOutput, calls=%fused_computation.8 | convolution fusion | flops 34359738368 | bytes 71303168 | tf_op jit(solution)/shard_map/dot_general | solution.py:20
  42.9 48.8 %fusion.25 = bf16[8192,1024]{1,0:T(8,128)(2,1)} fusion(bf16[2048,1024]{1,0:T(8,128)(2,1)} %param.8, bf16[8192,2048]{1,0:T(8,128)(2,1)} %param.6, f32[8192,1024]{1,0:T(8,128)} %fusion.1), kind=kOutput, calls=%bitcast_fusion.1.clone.1 | convolution fusion | flops 34410070016 | bytes 88080384 | tf_op jit(solution)/shard_map/dot_general | solution.py:21
  91.7 45.1 %convolution_convert_fusion = bf16[8192,2048]{1,0:T(8,128)(2,1)} fusion(bf16[1024,2048]{1,0:T(8,128)(2,1)} %param.9, bf16[8192,1024]{1,0:T(8,128)(2,1)} %fusion.25), kind=kOutput, calls=%fused_computation.2 | convolution fusion | flops 34376515584 | bytes 54525952 | tf_op jit(solution)/shard_map/dot_general | solution.py:23
  136.8 375.6 %all_to_all.9 = bf16[8,1024,2048]{2,1,0:T(8,128)(2,1)} all-to-all(bf16[8,1024,2048]{2,1,0:T(8,128)(2,1)} %bitcast.26), channel_id=1, replica_groups=mesh['data'=2,'tp'=8] {'tp'}, dimensions={0} | all-to-all | bytes 67108864 | tf_op jit(solution)/shard_map/all_to_all | solution.py:24
  512.4 15.0 %convert_reduce_fusion = f32[1024,2048]{1,0:T(8,128)} fusion(bf16[8,1024,2048]{2,1,0:T(8,128)(2,1)} %all_to_all.9), kind=kLoop, calls=%fused_computation | loop fusion | flops 31457280 | bytes 41943040 | tf_op jit(solution)/shard_map/reduce_sum | solution.py:26
  527.5 0.0 copy-start
  527.5 0.0 copy-start.1
  527.5 0.0 copy-start.2
  527.5 5.9 %multiply_reduce_fusion = f32[1024]{0:T(1024)S(1)} fusion(f32[1024,2048]{1,0:T(8,128)} %convert_reduce_fusion, bf16[1024,2048]{1,0:T(8,128)(2,1)} %param.10), kind=kLoop, calls=%fused_computation.4 | loop fusion | flops 8387584 | bytes 12587008 | tf_op jit(solution)/shard_map/reduce_sum | solution.py:11
  533.4 1.1 copy-done
  534.4 1.2 copy-done.1
  535.6 0.0 copy-done.2
  535.6 5.0 multiply_convert_fusion.1
  (1 shorter events, 0.0 us)
Async XLA Ops:
  527.5 7.0 %copy-start = (f32[1024,2048]{1,0:T(8,128)S(1)}, f32[1024,2048]{1,0:T(8,128)}, u32[]{:S(2)}) copy-start(f32[1024,2048]{1,0:T(8,128)} %convert_reduce_fusion) | copy-start | bytes 25165828
  527.5 8.2 %copy-start.1 = (bf16[1024,2048]{1,0:T(8,128)(2,1)S(1)}, bf16[1024,2048]{1,0:T(8,128)(2,1)}, u32[]{:S(2)}) copy-start(bf16[1024,2048]{1,0:T(8,128)(2,1)} %param.10) | copy-start | bytes 12582916
  527.5 8.2 %copy-start.2 = (f32[2048]{0:T(1024)S(1)}, f32[2048]{0:T(1024)}, u32[]{:S(2)}) copy-start(f32[2048]{0:T(1024)} %param.11) | copy-start | bytes 24580
where the time goes:
time: 541 us
  blocking collectives  376 us (70%)
  matrix products  136 us (25%)
  other arithmetic  25.9 us (5%)
    all_to_all x1, blocking collectives, local_block(): received = lax.all_to_all(part_prod, 'tp', 0, 0, tiled=True)  376 us
    dot_general x1, matrix products, local_block(): up_val = jnp.dot(x_in, w_up, preferred_element_type=jnp.float32)  48.8 us
    dot_general x1, matrix products, local_block(): jnp.dot(hidden, w_down, preferred_element_type=jnp.float32)  45.1 us
    dot_general x1, matrix products, local_block(): gate_val = jnp.dot(x_in, w_gate, preferred_element_type=jnp.float32)  42.3 us
    reduce_sum x1, other arithmetic, local_block(): jnp.sum(received.reshape(tp_size, rows, received.shape[1]), axis=0, dtype...  15 us

commit v1 on v0

v1 whole, which is shorter than its diff:
```python
import functools

import jax
import jax.numpy as jnp
from jax import lax
from jax.experimental import pallas as pl
from jax.experimental.pallas import tpu as pltpu
from jax.sharding import PartitionSpec as P

EPS = 1e-5
CORES = 2
ROWS = 128
SLOTS = 3
RIGHT, LEFT = 0, 1


def ring_kernel(
    n, x_in, w_gate, w_up, w_down, residual, h_out, mid_in, near_in,
    gate_w, up_w, down_w, x_tile, hidden, mid_out, stage, far_in, acc, extra, mid_tile, res_tile,
    w_sem, peer_send, peer_recv, x_sem, mid_send, mid_recv, stage_send, near_recv, far_recv, extra_sem, mid_sem, res_sem, out_sem,
):
    me = lax.axis_index("tp")
    chips = n // CORES
    chip, core = me // CORES, lax.rem(me, CORES)
    own_rows = residual.shape[0]
    half = own_rows // 2
    tiles = half // ROWS
    depth, width = w_gate.shape[1], w_down.shape[1]

    def device(c, k):
        return {"tp": lax.rem(c + chips, chips) * CORES + k}

    right, left, peer = device(chip + 1, core), device(chip - 1, core), device(chip, 1 - core)
    next_dev = (right, left)

    def x_copies(stg, t, slot):
        (c0, h0), (c1, h1) = (
            ((chip + 2, 0), (chip + 2, 1)),
            ((chip + 2, 0), (chip + 2, 1)),
            ((chip + 1, 1), (chip - 1, 0)),
            ((chip + 1, 0), (chip - 1, 1)),
            ((chip, 0), (chip, 1)),
        )[stg]
        out = []
        for d, (c, h) in enumerate(((c0, h0), (c1, h1))):
            c = lax.rem(c + chips, chips)
            row = pl.multiple_of((c * CORES + core) * own_rows + h * half + t * ROWS, ROWS)
            out.append(pltpu.make_async_copy(
                x_in.at[pl.ds(row, ROWS)], x_tile.at[slot, pl.ds(d * ROWS, ROWS)], x_sem.at[slot, d]))
        return out

    def start_x(stg, t, slot):
        for cp in x_copies(stg, t, slot):
            cp.start()

    def wait_x(stg, t, slot):
        for cp in x_copies(stg, t, slot):
            cp.wait()

    own_w = [
        pltpu.make_async_copy(w_gate, gate_w.at[0], w_sem.at[0]),
        pltpu.make_async_copy(w_up, up_w.at[0], w_sem.at[1]),
        pltpu.make_async_copy(w_down, down_w.at[0], w_sem.at[2]),
    ]
    start_x(0, 0, 0)
    for cp in own_w:
        cp.start()

    barrier = pltpu.get_barrier_semaphore()
    for dev in (peer, left, right):
        pl.semaphore_signal(barrier, inc=1, device_id=dev, device_id_type=pl.DeviceIdType.MESH)
    pl.semaphore_wait(barrier, 3)

    def remote(src, dst, send, recv, dev):
        return pltpu.make_async_remote_copy(
            src_ref=src, dst_ref=dst, send_sem=send, recv_sem=recv, device_id=dev, device_id_type=pl.DeviceIdType.MESH)

    peer_w = [
        remote(w_gate, gate_w.at[1], peer_send.at[0], peer_recv.at[0], peer),
        remote(w_up, up_w.at[1], peer_send.at[1], peer_recv.at[1], peer),
        remote(w_down, down_w.at[1], peer_send.at[2], peer_recv.at[2], peer),
    ]
    for cp in peer_w:
        cp.start()

    def rows_of(t):
        return pl.ds(pl.multiple_of(t * ROWS, ROWS), ROWS)

    def mid_copy(d, s, t):
        return remote(mid_out.at[s, d, rows_of(t)], mid_in.at[d, s, rows_of(t)],
                      mid_send.at[s, d, t], mid_recv.at[s, d, t], next_dev[d])

    def near_copy(d, t, slot):
        return remote(stage.at[slot, d], near_in.at[d, rows_of(t)], stage_send.at[slot, d], near_recv.at[d, t], next_dev[d])

    def far_copy(d, t, slot):
        return remote(stage.at[slot, d], far_in.at[d, rows_of(t)], stage_send.at[slot, d], far_recv.at[d, t], next_dev[d])

    def make_hidden(slot, s):
        def chunk(j, _):
            cols = pl.ds(pl.multiple_of(j * 256, 256), 256)
            x = x_tile[slot]
            gate = jnp.dot(x, gate_w[s, :, cols], preferred_element_type=jnp.float32)
            up = jnp.dot(x, up_w[s, :, cols], preferred_element_type=jnp.float32)
            hidden[s, :, cols] = (jax.nn.silu(gate) * up).astype(jnp.bfloat16)
            return 0
        lax.fori_loop(0, depth // 256, chunk, 0)

    def part(s, cols):
        return jnp.dot(hidden[s], down_w[s, :, cols], preferred_element_type=jnp.float32).astype(jnp.bfloat16)

    def both(slot, store):
        make_hidden(slot, 0)
        make_hidden(slot, 1)

        def chunk(j, _):
            cols = pl.ds(pl.multiple_of(j * 512, 512), 512)
            store(cols, part(0, cols).astype(jnp.float32) + part(1, cols).astype(jnp.float32))
            return 0
        lax.fori_loop(0, width // 512, chunk, 0)

    def next_x(stg, t, slot):
        @pl.when(t < tiles - 1)
        def _():
            start_x(stg, t + 1, 1 - slot)
        if stg < 4:
            @pl.when(t == tiles - 1)
            def _():
                start_x(stg + 1, 0, 1 - slot)

    for s in range(2):
        for w in range(3) if s == 0 else ():
            own_w[w].wait()
        if s == 1:
            for cp in peer_w:
                cp.wait_recv()

        def mid_step(t, _, s=s):
            slot = lax.rem(t, 2)
            next_x(s, t, slot)
            wait_x(s, t, slot)
            make_hidden(slot, s)

            def chunk(j, _):
                cols = pl.ds(pl.multiple_of(j * 512, 512), 512)
                y = part(s, cols)
                mid_out[s, RIGHT, rows_of(t), cols] = y[:ROWS]
                mid_out[s, LEFT, rows_of(t), cols] = y[ROWS:]
                return 0
            lax.fori_loop(0, width // 512, chunk, 0)
            for d in (RIGHT, LEFT):
                mid_copy(d, s, t).start()
            return 0
        lax.fori_loop(0, tiles, mid_step, 0)

    def near_step(t, _):
        slot, place = lax.rem(t, 2), lax.rem(t, SLOTS)
        next_x(2, t, slot)
        wait_x(2, t, slot)

        @pl.when(t >= SLOTS)
        def _():
            for d in (RIGHT, LEFT):
                near_copy(d, t - SLOTS, place).wait_send()

        def store(cols, y):
            stage[place, RIGHT, :, cols] = y[:ROWS]
            stage[place, LEFT, :, cols] = y[ROWS:]
        both(slot, store)
        for d in (RIGHT, LEFT):
            near_copy(d, t, place).start()
        return 0
    lax.fori_loop(0, tiles, near_step, 0)

    def mid_loads(t):
        return [pltpu.make_async_copy(mid_in.at[d, s, rows_of(t)], mid_tile.at[d, s], mid_sem.at[d, s])
                for d in (RIGHT, LEFT) for s in (0, 1)]

    def far_step(t, _):
        slot, place = lax.rem(t, 2), lax.rem(t + tiles, SLOTS)
        next_x(3, t, slot)
        wait_x(3, t, slot)
        for d in (RIGHT, LEFT):
            near_copy(d, t, place).wait_send()

        def store(cols, y):
            stage[place, RIGHT, :, cols] = y[:ROWS]
            stage[place, LEFT, :, cols] = y[ROWS:]
        both(slot, store)
        for d in (RIGHT, LEFT):
            for s in (0, 1):
                mid_copy(d, s, t).wait_recv()
        for cp in mid_loads(t):
            cp.start()
        for cp in mid_loads(t):
            cp.wait()

        def add(j, _):
            r = pl.ds(pl.multiple_of(j * 16, 16), 16)
            for d in (RIGHT, LEFT):
                stage[place, d, r] += mid_tile[d, 0, r].astype(jnp.float32) + mid_tile[d, 1, r].astype(jnp.float32)
            return 0
        lax.fori_loop(0, ROWS // 16, add, 0)
        for d in (RIGHT, LEFT):
            far_copy(d, t, place).start()
        return 0
    lax.fori_loop(0, tiles, far_step, 0)

    def own_loads(t):
        out = []
        for h in (0, 1):
            row = pl.multiple_of(h * half + t * ROWS, ROWS)
            out.append(pltpu.make_async_copy(near_in.at[1 - h, rows_of(t)], extra.at[h], extra_sem.at[h]))
            out.append(pltpu.make_async_copy(residual.at[pl.ds(row, ROWS)], res_tile.at[h], res_sem.at[h]))
        return out

    def own_step(t, _):
        slot = lax.rem(t, 2)
        next_x(4, t, slot)
        wait_x(4, t, slot)

        def store(cols, y):
            acc[0, rows_of(t), cols] = y[:ROWS]
            acc[1, rows_of(t), cols] = y[ROWS:]
        both(slot, store)
        for d in (RIGHT, LEFT):
            near_copy(d, t, 0).wait_recv()
        for cp in own_loads(t):
            cp.start()
        for cp in own_loads(t):
            cp.wait()

        def add(j, _):
            r = pl.ds(pl.multiple_of(j * 16, 16), 16)
            here = pl.ds(pl.multiple_of(t * ROWS + j * 16, 16), 16)
            for h in (0, 1):
                acc[h, here] += extra[h, r] + res_tile[h, r].astype(jnp.float32)
            return 0
        lax.fori_loop(0, ROWS // 16, add, 0)
        return 0
    lax.fori_loop(0, tiles, own_step, 0)

    def out_copies(t):
        return [pltpu.make_async_copy(
            acc.at[h, rows_of(t)], h_out.at[pl.ds(pl.multiple_of(h * half + t * ROWS, ROWS), ROWS)], out_sem.at[h, t])
            for h in (0, 1)]

    def last_step(t, _):
        for d in (RIGHT, LEFT):
            far_copy(d, t, 0).wait_recv()

        def add(j, _):
            here = pl.ds(pl.multiple_of(t * ROWS + j * 16, 16), 16)
            for h in (0, 1):
                acc[h, here] += far_in[h, here]
            return 0
        lax.fori_loop(0, ROWS // 16, add, 0)
        for cp in out_copies(t):
            cp.start()
        return 0
    lax.fori_loop(0, tiles, last_step, 0)

    for cp in peer_w:
        cp.wait_send()

    def drain(t, _):
        for d in (RIGHT, LEFT):
            for s in (0, 1):
                mid_copy(d, s, t).wait_send()
        for cp in out_copies(t):
            cp.wait()
        return 0
    lax.fori_loop(0, tiles, drain, 0)

    def drain_stage(i, _):
        for d in (RIGHT, LEFT):
            far_copy(d, 0, i).wait_send()
        return 0
    lax.fori_loop(0, SLOTS, drain_stage, 0)


def norm_kernel(h, gain, h_out, normed):
    value = h[...]
    mean_sq = jnp.mean(value * value, axis=-1, keepdims=True)
    h_out[...] = value.astype(jnp.bfloat16)
    normed[...] = (value * lax.rsqrt(mean_sq + EPS) * gain[...]).astype(jnp.bfloat16)


def solution(mesh):
    n = mesh.shape["tp"]

    def local_block(x_in, w_gate, w_up, w_down, residual, norm_gain):
        rows, width = residual.shape
        depth = w_gate.shape[1]
        half = rows // 2
        tiles = half // ROWS
        f32, bf16 = jnp.float32, jnp.bfloat16
        dma = pltpu.SemaphoreType.DMA
        h, _, _ = pl.pallas_call(
            functools.partial(ring_kernel, n),
            out_shape=(
                jax.ShapeDtypeStruct((rows, width), f32),
                jax.ShapeDtypeStruct((2, 2, half, width), bf16),
                jax.ShapeDtypeStruct((2, half, width), f32),
            ),
            in_specs=[pl.BlockSpec(memory_space=pl.ANY)] * 5,
            out_specs=(pl.BlockSpec(memory_space=pl.ANY),) * 3,
            scratch_shapes=[
                pltpu.VMEM((2,) + w_gate.shape, bf16),
                pltpu.VMEM((2,) + w_up.shape, bf16),
                pltpu.VMEM((2,) + w_down.shape, bf16),
                pltpu.VMEM((2, 2 * ROWS, width), bf16),
                pltpu.VMEM((2, 2 * ROWS, depth), bf16),
                pltpu.VMEM((2, 2, half, width), bf16),
                pltpu.VMEM((SLOTS, 2, ROWS, width), f32),
                pltpu.VMEM((2, half, width), f32),
                pltpu.VMEM((2, half, width), f32),
                pltpu.VMEM((2, ROWS, width), f32),
                pltpu.VMEM((2, 2, ROWS, width), bf16),
                pltpu.VMEM((2, ROWS, width), bf16),
                dma((3,)), dma((3,)), dma((3,)),
                dma((2, 2)),
                dma((2, 2, tiles)), dma((2, 2, tiles)),
                dma((SLOTS, 2)), dma((2, tiles)), dma((2, tiles)),
                dma((2,)), dma((2, 2)), dma((2,)), dma((2, tiles)),
            ],
            compiler_params=pltpu.CompilerParams(
                collective_id=0, has_side_effects=True, vmem_limit_bytes=66_000_000),
            name="ring",
        )(x_in, w_gate, w_up, w_down, residual)
        row_block = pl.BlockSpec((ROWS, width), lambda i: (i, 0))
        return pl.pallas_call(
            norm_kernel,
            grid=(rows // ROWS,),
            out_shape=(jax.ShapeDtypeStruct((rows, width), bf16),) * 2,
            in_specs=[row_block, pl.BlockSpec((1, width), lambda i: (0, 0))],
            out_specs=(row_block, row_block),
            name="norm",
        )(h, norm_gain.reshape(1, width))

    row_spec = P(("data", "tp"), None)
    return jax.shard_map(local_block, mesh=mesh, in_specs=(P("data", None), P(None, "tp"), P(None, "tp"), P("tp", None), row_spec, P(None)), out_specs=(row_spec, row_spec), check_vma=False)
```

time: 541 us -> 296 us (0.55)
  blocking collectives: 376 us -> 0 us
  Pallas kernels: 0 us -> 295 us
  matrix products: 136 us -> 0 us
  other arithmetic: 25.9 us -> 0 us
    all_to_all x1 -> x0, blocking collectives: 376 us -> none  [local_block(): received = lax.all_to_all(part_prod, 'tp', 0, 0, tiled=True)]
    pallas_call x0 -> x2, Pallas kernels: none -> 295 us  [the longest x1 286 us: local_block(): pl.pallas_call(functools.partial(ring_kernel, n), out_shape=(jax.ShapeDty...]
    dot_general x3 -> x0, matrix products: 136 us -> none  [the longest x1 48.8 us: local_block(): up_val = jnp.dot(x_in, w_up, preferred_element_type=jnp.float32)]
    reduce_sum x2 -> x0, other arithmetic: 20.9 us -> none  [the longest x1 15 us: local_block(): jnp.sum(received.reshape(tp_size, rows, received.shape[1]), axis=0, dtype...]
where the time goes in v1:
time: 296 us
  Pallas kernels  295 us (100%)
    pallas_call x1, Pallas kernels, local_block(): pl.pallas_call(functools.partial(ring_kernel, n), out_shape=(jax.ShapeDty...  286 us
    pallas_call x1, Pallas kernels, local_block(): pl.pallas_call(norm_kernel, grid=(rows // ROWS,), out_shape=(jax.ShapeDty...  8.95 us

profile of v1, /device:TPU:112, one launch (start us, length us, event | category | flops | bytes accessed | tf_op | source)
XLA Modules:
  0.0 296.0 jit_solution(2982121190560508474)
XLA Ops:
  0.6 286.4 %ring.1 = (f32[1024,2048]{1,0:T(8,128)}, bf16[2,2,512,2048]{3,2,1,0:T(8,128)(2,1)}, f32[2,512,2048]{2,1,0:T(8,128)}) custom-call(bf16[8192,2048]{1,0:T(8,128)(2,1)} %x_in.1, bf16[2048,1024]{1,0:T(8,128)(2,1)} %w_gate.1, bf16[2048,1024]{1,0:T(8,128)(2,1)} %w_up.1, bf16[1024,2048]{1,0:T(8,128)(2,1)} %w_down.1, bf16[1024,2048]{1,0:T(8,128)(2,1)} %residual.1), custom_call_target="tpu_custom_call" | custom-call | tf_op jit(solution)/shard_map/ring/pallas_call | solution.py:299
  287.0 9.0 %norm.1 = (bf16[1024,2048]{1,0:T(8,128)(2,1)}, bf16[1024,2048]{1,0:T(8,128)(2,1)}) custom-call(f32[1024,2048]{1,0:T(8,128)} %get-tuple-element.3.h, f32[1,2048]{1,0:T(1,128)} %bitcast.1), custom_call_target="tpu_custom_call" | custom-call | tf_op jit(solution)/shard_map/norm/pallas_call | solution.py:332

commit v2 on v1

--- a/solution.py
+++ b/solution.py
@@ -11,13 +11,16 @@
 CORES = 2
 ROWS = 128
 SLOTS = 3
+SUB = 32
+WCOLS = 256
 RIGHT, LEFT = 0, 1
 
 
 def ring_kernel(
-    n, x_in, w_gate, w_up, w_down, residual, h_out, mid_in, near_in,
-    gate_w, up_w, down_w, x_tile, hidden, mid_out, stage, far_in, acc, extra, mid_tile, res_tile,
-    w_sem, peer_send, peer_recv, x_sem, mid_send, mid_recv, stage_send, near_recv, far_recv, extra_sem, mid_sem, res_sem, out_sem,
+    n, x_in, w_gate, w_up, w_down, residual, norm_gain, result, mid_in, near_in,
+    gate_w, up_w, down_w, x_tile, hidden, stage, far_in, acc, extra, mid_tile, res_tile, gain,
+    gate_sem, up_sem, down_sem, peer_send, peer_recv, x_sem, mid_send, mid_recv, stage_send, near_recv, far_recv, last_send,
+    last_recv, extra_sem, mid_sem, res_sem, gain_sem,
 ):
     me = lax.axis_index("tp")
     chips = n // CORES
@@ -32,6 +35,7 @@
 
     right, left, peer = device(chip + 1, core), device(chip - 1, core), device(chip, 1 - core)
     next_dev = (right, left)
+    last_place = (2 * tiles - 1) % SLOTS
 
     def x_copies(stg, t, slot):
         (c0, h0), (c1, h1) = (
@@ -57,14 +61,21 @@
         for cp in x_copies(stg, t, slot):
             cp.wait()
 
-    own_w = [
-        pltpu.make_async_copy(w_gate, gate_w.at[0], w_sem.at[0]),
-        pltpu.make_async_copy(w_up, up_w.at[0], w_sem.at[1]),
-        pltpu.make_async_copy(w_down, down_w.at[0], w_sem.at[2]),
-    ]
+    def own_cols(j):
+        cols = pl.ds(pl.multiple_of(j * WCOLS, WCOLS), WCOLS)
+        return [
+            pltpu.make_async_copy(w_gate.at[:, cols], gate_w.at[0, :, cols], gate_sem.at[j]),
+            pltpu.make_async_copy(w_up.at[:, cols], up_w.at[0, :, cols], up_sem.at[j]),
+        ]
+
+    own_down = pltpu.make_async_copy(w_down, down_w.at[0], down_sem)
+    own_gain = pltpu.make_async_copy(norm_gain, gain, gain_sem)
     start_x(0, 0, 0)
-    for cp in own_w:
-        cp.start()
+    for j in range(depth // WCOLS):
+        for cp in own_cols(j):
+            cp.start()
+    own_down.start()
+    own_gain.start()
 
     barrier = pltpu.get_barrier_semaphore()
     for dev in (peer, left, right):
@@ -87,7 +98,7 @@
         return pl.ds(pl.multiple_of(t * ROWS, ROWS), ROWS)
 
     def mid_copy(d, s, t):
-        return remote(mid_out.at[s, d, rows_of(t)], mid_in.at[d, s, rows_of(t)],
+        return remote(result.at[s, d, rows_of(t)], mid_in.at[d, s, rows_of(t)],
                       mid_send.at[s, d, t], mid_recv.at[s, d, t], next_dev[d])
 
     def near_copy(d, t, slot):
@@ -96,15 +107,23 @@
     def far_copy(d, t, slot):
         return remote(stage.at[slot, d], far_in.at[d, rows_of(t)], stage_send.at[slot, d], far_recv.at[d, t], next_dev[d])
 
-    def make_hidden(slot, s):
+    def last_copy(d, i):
+        here = pl.ds((tiles - 1) * ROWS + i * SUB, SUB)
+        return remote(stage.at[last_place, d, pl.ds(i * SUB, SUB)], far_in.at[d, here],
+                      last_send.at[d, i], last_recv.at[d, i], next_dev[d])
+
+    def make_hidden(slot, s, first=False):
         def chunk(j, _):
-            cols = pl.ds(pl.multiple_of(j * 256, 256), 256)
+            if first:
+                for cp in own_cols(j):
+                    cp.wait()
+            cols = pl.ds(pl.multiple_of(j * WCOLS, WCOLS), WCOLS)
             x = x_tile[slot]
             gate = jnp.dot(x, gate_w[s, :, cols], preferred_element_type=jnp.float32)
             up = jnp.dot(x, up_w[s, :, cols], preferred_element_type=jnp.float32)
             hidden[s, :, cols] = (jax.nn.silu(gate) * up).astype(jnp.bfloat16)
             return 0
-        lax.fori_loop(0, depth // 256, chunk, 0)
+        lax.fori_loop(0, depth // WCOLS, chunk, 0)
 
     def part(s, cols):
         return jnp.dot(hidden[s], down_w[s, :, cols], preferred_element_type=jnp.float32).astype(jnp.bfloat16)
@@ -128,30 +147,36 @@
             def _():
                 start_x(stg + 1, 0, 1 - slot)
 
-    for s in range(2):
-        for w in range(3) if s == 0 else ():
-            own_w[w].wait()
-        if s == 1:
-            for cp in peer_w:
-                cp.wait_recv()
-
-        def mid_step(t, _, s=s):
+    def mid_step(t, s, first=False):
             slot = lax.rem(t, 2)
             next_x(s, t, slot)
             wait_x(s, t, slot)
-            make_hidden(slot, s)
+            make_hidden(slot, s, first)
+            if first:
+                own_down.wait()
 
             def chunk(j, _):
                 cols = pl.ds(pl.multiple_of(j * 512, 512), 512)
                 y = part(s, cols)
-                mid_out[s, RIGHT, rows_of(t), cols] = y[:ROWS]
-                mid_out[s, LEFT, rows_of(t), cols] = y[ROWS:]
+                result[s, RIGHT, rows_of(t), cols] = y[:ROWS]
+                result[s, LEFT, rows_of(t), cols] = y[ROWS:]
                 return 0
             lax.fori_loop(0, width // 512, chunk, 0)
             for d in (RIGHT, LEFT):
                 mid_copy(d, s, t).start()
-            return 0
-        lax.fori_loop(0, tiles, mid_step, 0)
+
+    mid_step(jnp.int32(0), 0, first=True)
+
+    def mid_loop(s, t0):
+        def step(t, _):
+            mid_step(t, s)
+            return 0
+        lax.fori_loop(t0, tiles, step, 0)
+
+    mid_loop(0, 1)
+    for cp in peer_w:
+        cp.wait_recv()
+    mid_loop(1, 0)
 
     def near_step(t, _):
         slot, place = lax.rem(t, 2), lax.rem(t, SLOTS)
@@ -201,8 +226,17 @@
                 stage[place, d, r] += mid_tile[d, 0, r].astype(jnp.float32) + mid_tile[d, 1, r].astype(jnp.float32)
             return 0
         lax.fori_loop(0, ROWS // 16, add, 0)
-        for d in (RIGHT, LEFT):
-            far_copy(d, t, place).start()
+
+        @pl.when(t < tiles - 1)
+        def _():
+            for d in (RIGHT, LEFT):
+                far_copy(d, t, place).start()
+
+        @pl.when(t == tiles - 1)
+        def _():
+            for i in range(ROWS // SUB):
+                for d in (RIGHT, LEFT):
+                    last_copy(d, i).start()
         return 0
     lax.fori_loop(0, tiles, far_step, 0)
 
@@ -240,26 +274,6 @@
         return 0
     lax.fori_loop(0, tiles, own_step, 0)
 
-    def out_copies(t):
-        return [pltpu.make_async_copy(
-            acc.at[h, rows_of(t)], h_out.at[pl.ds(pl.multiple_of(h * half + t * ROWS, ROWS), ROWS)], out_sem.at[h, t])
-            for h in (0, 1)]
-
-    def last_step(t, _):
-        for d in (RIGHT, LEFT):
-            far_copy(d, t, 0).wait_recv()
-
-        def add(j, _):
-            here = pl.ds(pl.multiple_of(t * ROWS + j * 16, 16), 16)
-            for h in (0, 1):
-                acc[h, here] += far_in[h, here]
-            return 0
-        lax.fori_loop(0, ROWS // 16, add, 0)
-        for cp in out_copies(t):
-            cp.start()
-        return 0
-    lax.fori_loop(0, tiles, last_step, 0)
-
     for cp in peer_w:
         cp.wait_send()
 
@@ -267,23 +281,53 @@
         for d in (RIGHT, LEFT):
             for s in (0, 1):
                 mid_copy(d, s, t).wait_send()
-        for cp in out_copies(t):
-            cp.wait()
         return 0
     lax.fori_loop(0, tiles, drain, 0)
-
-    def drain_stage(i, _):
-        for d in (RIGHT, LEFT):
-            far_copy(d, 0, i).wait_send()
-        return 0
-    lax.fori_loop(0, SLOTS, drain_stage, 0)
-
-
-def norm_kernel(h, gain, h_out, normed):
-    value = h[...]
-    mean_sq = jnp.mean(value * value, axis=-1, keepdims=True)
-    h_out[...] = value.astype(jnp.bfloat16)
-    normed[...] = (value * lax.rsqrt(mean_sq + EPS) * gain[...]).astype(jnp.bfloat16)
+    own_gain.wait()
+
+    def finish(row):
+        for h in (0, 1):
+            here = pl.ds(row, 16)
+            value = acc[h, here] + far_in[h, here]
+            mean_sq = jnp.mean(value * value, axis=-1, keepdims=True)
+            result[0, h, here] = value.astype(jnp.bfloat16)
+            result[1, h, here] = (value * lax.rsqrt(mean_sq + EPS) * gain[...]).astype(jnp.bfloat16)
+
+    def last_step(t, _):
+        for d in (RIGHT, LEFT):
+            far_copy(d, t, 0).wait_recv()
+
+        def rows16(j, _):
+            finish(pl.multiple_of(t * ROWS + j * 16, 16))
+            return 0
+        lax.fori_loop(0, ROWS // 16, rows16, 0)
+        return 0
+    lax.fori_loop(0, tiles - 1, last_step, 0)
+
+    for place in range(SLOTS):
+        if place != last_place:
+            for d in (RIGHT, LEFT):
+                far_copy(d, 0, place).wait_send()
+
+    for i in range(ROWS // SUB):
+        for d in (RIGHT, LEFT):
+            last_copy(d, i).wait_recv()
+        for j in range(SUB // 16):
+            finish((tiles - 1) * ROWS + i * SUB + j * 16)
+    for i in range(ROWS // SUB):
+        for d in (RIGHT, LEFT):
+            last_copy(d, i).wait_send()
+
+
+def write_kernel(result, h_out, normed, sem):
+    half = result.shape[2]
+    copies = [
+        pltpu.make_async_copy(result.at[i, h], out.at[pl.ds(h * half, half)], sem.at[i, h])
+        for i, out in enumerate((h_out, normed)) for h in (0, 1)]
+    for cp in copies:
+        cp.start()
+    for cp in copies:
+        cp.wait()
 
 
 def solution(mesh):
@@ -296,47 +340,49 @@
         tiles = half // ROWS
         f32, bf16 = jnp.float32, jnp.bfloat16
         dma = pltpu.SemaphoreType.DMA
-        h, _, _ = pl.pallas_call(
+        any_space = pl.BlockSpec(memory_space=pl.ANY)
+        result, _, _ = pl.pallas_call(
             functools.partial(ring_kernel, n),
             out_shape=(
-                jax.ShapeDtypeStruct((rows, width), f32),
+                pltpu.VMEM((2, 2, half, width), bf16),
                 jax.ShapeDtypeStruct((2, 2, half, width), bf16),
                 jax.ShapeDtypeStruct((2, half, width), f32),
             ),
-            in_specs=[pl.BlockSpec(memory_space=pl.ANY)] * 5,
-            out_specs=(pl.BlockSpec(memory_space=pl.ANY),) * 3,
+            in_specs=[any_space] * 6,
+            out_specs=(pl.BlockSpec(memory_space=pltpu.VMEM), any_space, any_space),
             scratch_shapes=[
                 pltpu.VMEM((2,) + w_gate.shape, bf16),
                 pltpu.VMEM((2,) + w_up.shape, bf16),
                 pltpu.VMEM((2,) + w_down.shape, bf16),
                 pltpu.VMEM((2, 2 * ROWS, width), bf16),
                 pltpu.VMEM((2, 2 * ROWS, depth), bf16),
-                pltpu.VMEM((2, 2, half, width), bf16),
                 pltpu.VMEM((SLOTS, 2, ROWS, width), f32),
                 pltpu.VMEM((2, half, width), f32),
                 pltpu.VMEM((2, half, width), f32),
                 pltpu.VMEM((2, ROWS, width), f32),
                 pltpu.VMEM((2, 2, ROWS, width), bf16),
                 pltpu.VMEM((2, ROWS, width), bf16),
-                dma((3,)), dma((3,)), dma((3,)),
+                pltpu.VMEM((1, width), f32),
+                dma((depth // WCOLS,)), dma((depth // WCOLS,)), dma(()), dma((3,)), dma((3,)),
                 dma((2, 2)),
                 dma((2, 2, tiles)), dma((2, 2, tiles)),
                 dma((SLOTS, 2)), dma((2, tiles)), dma((2, tiles)),
-                dma((2,)), dma((2, 2)), dma((2,)), dma((2, tiles)),
+                dma((2, ROWS // SUB)), dma((2, ROWS // SUB)),
+                dma((2,)), dma((2, 2)), dma((2,)), dma(()),
             ],
             compiler_params=pltpu.CompilerParams(
-                collective_id=0, has_side_effects=True, vmem_limit_bytes=66_000_000),
+                collective_id=0, has_side_effects=True, vmem_limit_bytes=55 * 2**20),
             name="ring",
-        )(x_in, w_gate, w_up, w_down, residual)
-        row_block = pl.BlockSpec((ROWS, width), lambda i: (i, 0))
+        )(x_in, w_gate, w_up, w_down, residual, norm_gain.reshape(1, width))
         return pl.pallas_call(
-            norm_kernel,
-            grid=(rows // ROWS,),
+            write_kernel,
             out_shape=(jax.ShapeDtypeStruct((rows, width), bf16),) * 2,
-            in_specs=[row_block, pl.BlockSpec((1, width), lambda i: (0, 0))],
-            out_specs=(row_block, row_block),
-            name="norm",
-        )(h, norm_gain.reshape(1, width))
+            in_specs=[pl.BlockSpec(memory_space=pltpu.VMEM)],
+            out_specs=(any_space, any_space),
+            scratch_shapes=[dma((2, 2))],
+            compiler_params=pltpu.CompilerParams(vmem_limit_bytes=2**20),
+            name="write",
+        )(pltpu.with_memory_space_constraint(result, pltpu.VMEM))
 
     row_spec = P(("data", "tp"), None)
     return jax.shard_map(local_block, mesh=mesh, in_specs=(P("data", None), P(None, "tp"), P(None, "tp"), P("tp", None), row_spec, P(None)), out_specs=(row_spec, row_spec), check_vma=False)

time: 296 us -> 288 us (0.973)
  Pallas kernels: 295 us -> 287 us
    pallas_call x2, Pallas kernels: 295 us -> 287 us  [the longest x1 283 us: local_block(): pl.pallas_call(functools.partial(ring_kernel, n), out_shape=(pltpu.VMEM((...]
where the time goes in v2:
time: 288 us; the launch traced here: 287 us
  Pallas kernels  287 us (100%)
    pallas_call x1, Pallas kernels, local_block(): pl.pallas_call(functools.partial(ring_kernel, n), out_shape=(pltpu.VMEM((...  283 us

profile of v2, /device:TPU:112, one launch (start us, length us, event | category | flops | bytes accessed | tf_op | source)
XLA Modules:
  0.0 287.4 jit_solution(92767326100883629)
XLA Ops:
  0.6 283.3 %ring.1 = (bf16[2,2,512,2048]{3,2,1,0:T(8,128)(2,1)S(1)}, bf16[2,2,512,2048]{3,2,1,0:T(8,128)(2,1)}, f32[2,512,2048]{2,1,0:T(8,128)}) custom-call(bf16[8192,2048]{1,0:T(8,128)(2,1)} %x_in.1, bf16[2048,1024]{1,0:T(8,128)(2,1)} %w_gate.1, bf16[2048,1024]{1,0:T(8,128)(2,1)} %w_up.1, bf16[1024,2048]{1,0:T(8,128)(2,1)} %w_down.1, bf16[1024,2048]{1,0:T(8,128)(2,1)} %residual.1, ...), custom_call_target="tpu_custom_call" | custom-call | tf_op jit(solution)/shard_map/ring/pallas_call | solution.py:344
  284.0 3.4 %write.1 = (bf16[1024,2048]{1,0:T(8,128)(2,1)}, bf16[1024,2048]{1,0:T(8,128)(2,1)}) custom-call(bf16[2,2,512,2048]{3,2,1,0:T(8,128)(2,1)S(1)} %get-tuple-element.3.result), custom_call_target="tpu_custom_call" | custom-call | tf_op jit(solution)/shard_map/write/pallas_call | solution.py:377

commit v3 on v2

--- a/solution.py
+++ b/solution.py
@@ -12,7 +12,10 @@
 ROWS = 128
 SLOTS = 3
 SUB = 32
+FIRST = 64
 WCOLS = 256
+YCOLS = 512
+AHEAD = 4
 RIGHT, LEFT = 0, 1
 
 
@@ -20,7 +23,7 @@
     n, x_in, w_gate, w_up, w_down, residual, norm_gain, result, mid_in, near_in,
     gate_w, up_w, down_w, x_tile, hidden, stage, far_in, acc, extra, mid_tile, res_tile, gain,
     gate_sem, up_sem, down_sem, peer_send, peer_recv, x_sem, mid_send, mid_recv, stage_send, near_recv, far_recv, last_send,
-    last_recv, extra_sem, mid_sem, res_sem, gain_sem,
+    last_recv, extra_sem, mid_sem, res_sem, gain_sem, piece_sem, piece_send, piece_recv,
 ):
     me = lax.axis_index("tp")
     chips = n // CORES
@@ -61,6 +64,14 @@
         for cp in x_copies(stg, t, slot):
             cp.wait()
 
+    def piece_copies(i):
+        out = []
+        for d in (RIGHT, LEFT):
+            row = pl.multiple_of((lax.rem(chip + 2, chips) * CORES + core) * own_rows + d * half + i * FIRST, FIRST)
+            out.append(pltpu.make_async_copy(
+                x_in.at[pl.ds(row, FIRST)], x_tile.at[0, pl.ds((2 * i + d) * FIRST, FIRST)], piece_sem.at[i, d]))
+        return out
+
     def own_cols(j):
         cols = pl.ds(pl.multiple_of(j * WCOLS, WCOLS), WCOLS)
         return [
@@ -68,19 +79,33 @@
             pltpu.make_async_copy(w_up.at[:, cols], up_w.at[0, :, cols], up_sem.at[j]),
         ]
 
-    own_down = pltpu.make_async_copy(w_down, down_w.at[0], down_sem)
+    def own_down(j):
+        cols = pl.ds(pl.multiple_of(j * YCOLS, YCOLS), YCOLS)
+        return pltpu.make_async_copy(w_down.at[:, cols], down_w.at[0, :, cols], down_sem.at[j])
+
     own_gain = pltpu.make_async_copy(norm_gain, gain, gain_sem)
-    start_x(0, 0, 0)
-    for j in range(depth // WCOLS):
-        for cp in own_cols(j):
+    loads = [own_cols(j) for j in range(depth // WCOLS)] + [[own_down(j)] for j in range(width // YCOLS)]
+
+    def start_load(i):
+        for cp in loads[i] if i < len(loads) else ():
             cp.start()
-    own_down.start()
-    own_gain.start()
+
+    def wait_load(i):
+        for cp in loads[i]:
+            cp.wait()
+        start_load(i + AHEAD)
+
+    for cp in piece_copies(0):
+        cp.start()
+    for i in range(AHEAD):
+        start_load(i)
+    for k in range(1, ROWS // FIRST):
+        for cp in piece_copies(k):
+            cp.start()
 
     barrier = pltpu.get_barrier_semaphore()
     for dev in (peer, left, right):
         pl.semaphore_signal(barrier, inc=1, device_id=dev, device_id_type=pl.DeviceIdType.MESH)
-    pl.semaphore_wait(barrier, 3)
 
     def remote(src, dst, send, recv, dev):
         return pltpu.make_async_remote_copy(
@@ -91,8 +116,6 @@
         remote(w_up, up_w.at[1], peer_send.at[1], peer_recv.at[1], peer),
         remote(w_down, down_w.at[1], peer_send.at[2], peer_recv.at[2], peer),
     ]
-    for cp in peer_w:
-        cp.start()
 
     def rows_of(t):
         return pl.ds(pl.multiple_of(t * ROWS, ROWS), ROWS)
@@ -112,31 +135,43 @@
         return remote(stage.at[last_place, d, pl.ds(i * SUB, SUB)], far_in.at[d, here],
                       last_send.at[d, i], last_recv.at[d, i], next_dev[d])
 
-    def make_hidden(slot, s, first=False):
+    def piece_copy(d, i, j):
+        here, cols = pl.ds(i * FIRST, FIRST), pl.ds(j * YCOLS, YCOLS)
+        return remote(result.at[0, d, here, cols], mid_in.at[d, 0, here, cols],
+                      piece_send.at[d, i, j], piece_recv.at[d, i, j], next_dev[d])
+
+    pieces = [(d, i, j) for i in range(ROWS // FIRST) for j in range(width // YCOLS) for d in (RIGHT, LEFT)]
+
+    def make_hidden(slot, s, piece=None):
+        rows = pl.ds(0, 2 * ROWS) if piece is None else pl.ds(piece * 2 * FIRST, 2 * FIRST)
+
         def chunk(j, _):
-            if first:
-                for cp in own_cols(j):
-                    cp.wait()
+            if piece == 0:
+                wait_load(j)
             cols = pl.ds(pl.multiple_of(j * WCOLS, WCOLS), WCOLS)
-            x = x_tile[slot]
+            x = x_tile[slot, rows]
             gate = jnp.dot(x, gate_w[s, :, cols], preferred_element_type=jnp.float32)
             up = jnp.dot(x, up_w[s, :, cols], preferred_element_type=jnp.float32)
-            hidden[s, :, cols] = (jax.nn.silu(gate) * up).astype(jnp.bfloat16)
-            return 0
-        lax.fori_loop(0, depth // WCOLS, chunk, 0)
-
-    def part(s, cols):
-        return jnp.dot(hidden[s], down_w[s, :, cols], preferred_element_type=jnp.float32).astype(jnp.bfloat16)
+            hidden[s, rows, cols] = (jax.nn.silu(gate) * up).astype(jnp.bfloat16)
+            return 0
+        if piece == 0:
+            for j in range(depth // WCOLS):
+                chunk(j, 0)
+        else:
+            lax.fori_loop(0, depth // WCOLS, chunk, 0)
+
+    def part(s, cols, rows=pl.ds(0, 2 * ROWS)):
+        return jnp.dot(hidden[s, rows], down_w[s, :, cols], preferred_element_type=jnp.float32).astype(jnp.bfloat16)
 
     def both(slot, store):
         make_hidden(slot, 0)
         make_hidden(slot, 1)
 
         def chunk(j, _):
-            cols = pl.ds(pl.multiple_of(j * 512, 512), 512)
+            cols = pl.ds(pl.multiple_of(j * YCOLS, YCOLS), YCOLS)
             store(cols, part(0, cols).astype(jnp.float32) + part(1, cols).astype(jnp.float32))
             return 0
-        lax.fori_loop(0, width // 512, chunk, 0)
+        lax.fori_loop(0, width // YCOLS, chunk, 0)
 
     def next_x(stg, t, slot):
         @pl.when(t < tiles - 1)
@@ -147,25 +182,45 @@
             def _():
                 start_x(stg + 1, 0, 1 - slot)
 
-    def mid_step(t, s, first=False):
+    def mid_step(t, s):
             slot = lax.rem(t, 2)
             next_x(s, t, slot)
             wait_x(s, t, slot)
-            make_hidden(slot, s, first)
-            if first:
-                own_down.wait()
+            make_hidden(slot, s)
 
             def chunk(j, _):
-                cols = pl.ds(pl.multiple_of(j * 512, 512), 512)
+                cols = pl.ds(pl.multiple_of(j * YCOLS, YCOLS), YCOLS)
                 y = part(s, cols)
                 result[s, RIGHT, rows_of(t), cols] = y[:ROWS]
                 result[s, LEFT, rows_of(t), cols] = y[ROWS:]
                 return 0
-            lax.fori_loop(0, width // 512, chunk, 0)
+            lax.fori_loop(0, width // YCOLS, chunk, 0)
             for d in (RIGHT, LEFT):
                 mid_copy(d, s, t).start()
 
-    mid_step(jnp.int32(0), 0, first=True)
+    for i in range(ROWS // FIRST):
+        for cp in piece_copies(i):
+            cp.wait()
+        make_hidden(0, 0, piece=i)
+        if i == 0:
+            pl.semaphore_wait(barrier, 3)
+
+        def piece_chunk(j, i=i):
+            if i == 0:
+                wait_load(depth // WCOLS + j)
+            cols = pl.ds(pl.multiple_of(j * YCOLS, YCOLS), YCOLS)
+            y = part(0, cols, pl.ds(i * 2 * FIRST, 2 * FIRST))
+            for d in (RIGHT, LEFT):
+                result[0, d, pl.ds(i * FIRST, FIRST), cols] = y[d * FIRST:(d + 1) * FIRST]
+            for d in (RIGHT, LEFT):
+                piece_copy(d, i, j).start()
+        for j in range(width // YCOLS):
+            piece_chunk(j)
+        if i == 0:
+            own_gain.start()
+            for cp in peer_w:
+                cp.start()
+            start_x(0, 1, 1)
 
     def mid_loop(s, t0):
         def step(t, _):
@@ -213,8 +268,17 @@
             stage[place, LEFT, :, cols] = y[ROWS:]
         both(slot, store)
         for d in (RIGHT, LEFT):
-            for s in (0, 1):
-                mid_copy(d, s, t).wait_recv()
+            mid_copy(d, 1, t).wait_recv()
+
+        @pl.when(t == 0)
+        def _():
+            for piece in pieces:
+                piece_copy(*piece).wait_recv()
+
+        @pl.when(t > 0)
+        def _():
+            for d in (RIGHT, LEFT):
+                mid_copy(d, 0, t).wait_recv()
         for cp in mid_loads(t):
             cp.start()
         for cp in mid_loads(t):
@@ -277,10 +341,17 @@
     for cp in peer_w:
         cp.wait_send()
 
+    for piece in pieces:
+        piece_copy(*piece).wait_send()
+
     def drain(t, _):
         for d in (RIGHT, LEFT):
-            for s in (0, 1):
-                mid_copy(d, s, t).wait_send()
+            mid_copy(d, 1, t).wait_send()
+
+        @pl.when(t > 0)
+        def _():
+            for d in (RIGHT, LEFT):
+                mid_copy(d, 0, t).wait_send()
         return 0
     lax.fori_loop(0, tiles, drain, 0)
     own_gain.wait()
@@ -363,12 +434,13 @@
                 pltpu.VMEM((2, 2, ROWS, width), bf16),
                 pltpu.VMEM((2, ROWS, width), bf16),
                 pltpu.VMEM((1, width), f32),
-                dma((depth // WCOLS,)), dma((depth // WCOLS,)), dma(()), dma((3,)), dma((3,)),
+                dma((depth // WCOLS,)), dma((depth // WCOLS,)), dma((width // YCOLS,)), dma((3,)), dma((3,)),
                 dma((2, 2)),
                 dma((2, 2, tiles)), dma((2, 2, tiles)),
                 dma((SLOTS, 2)), dma((2, tiles)), dma((2, tiles)),
                 dma((2, ROWS // SUB)), dma((2, ROWS // SUB)),
                 dma((2,)), dma((2, 2)), dma((2,)), dma(()),
+                dma((ROWS // FIRST, 2)), dma((2, ROWS // FIRST, width // YCOLS)), dma((2, ROWS // FIRST, width // YCOLS)),
             ],
             compiler_params=pltpu.CompilerParams(
                 collective_id=0, has_side_effects=True, vmem_limit_bytes=55 * 2**20),

time: 288 us -> 285 us (0.990)
  Pallas kernels: 287 us -> 284 us
    pallas_call x1, Pallas kernels: 283 us -> 280 us  [local_block(): pl.pallas_call(functools.partial(ring_kernel, n), out_shape=(pltpu.VMEM((...]
where the time goes in v3:
time: 285 us; the launch traced here: 284 us
  Pallas kernels  284 us (100%)
    pallas_call x1, Pallas kernels, local_block(): pl.pallas_call(functools.partial(ring_kernel, n), out_shape=(pltpu.VMEM((...  280 us

profile of v3, /device:TPU:112, one launch (start us, length us, event | category | flops | bytes accessed | tf_op | source)
XLA Modules:
  0.0 284.4 jit_solution(5274640414338607113)
XLA Ops:
  0.6 280.4 %ring.1 = (bf16[2,2,512,2048]{3,2,1,0:T(8,128)(2,1)S(1)}, bf16[2,2,512,2048]{3,2,1,0:T(8,128)(2,1)}, f32[2,512,2048]{2,1,0:T(8,128)}) custom-call(bf16[8192,2048]{1,0:T(8,128)(2,1)} %x_in.1, bf16[2048,1024]{1,0:T(8,128)(2,1)} %w_gate.1, bf16[2048,1024]{1,0:T(8,128)(2,1)} %w_up.1, bf16[1024,2048]{1,0:T(8,128)(2,1)} %w_down.1, bf16[1024,2048]{1,0:T(8,128)(2,1)} %residual.1, ...), custom_call_target="tpu_custom_call" | custom-call | tf_op jit(solution)/shard_map/ring/pallas_call | solution.py:415
  281.0 3.4 %write.1 = (bf16[1024,2048]{1,0:T(8,128)(2,1)}, bf16[1024,2048]{1,0:T(8,128)(2,1)}) custom-call(bf16[2,2,512,2048]{3,2,1,0:T(8,128)(2,1)S(1)} %get-tuple-element.3.result), custom_call_target="tpu_custom_call" | custom-call | tf_op jit(solution)/shard_map/write/pallas_call | solution.py:449

commit v4 on v3

v4 whole, which is shorter than its diff:
```python
import functools

import jax
import jax.numpy as jnp
from jax import lax
from jax.experimental import pallas as pl
from jax.experimental.pallas import tpu as pltpu
from jax.sharding import PartitionSpec as P

EPS = 1e-5
CORES = 2
ROWS = 128
FAR_SLOTS, NEAR_SLOTS = 3, 2
SUB = 32
FIRST = 64
WCOLS = 256
YCOLS = 512
AHEAD = 4
RIGHT, LEFT = 0, 1
VMEM_LIMIT = 58_500_000


def ring_kernel(
    n, x_in, w_gate, w_up, w_down, residual, norm_gain, result, y_in, g_in, down_in,
    gate_w, up_w, down_w, x_tile, hidden, near_y, near_g, stage, far_in, acc, y_tile, g_tile, gain,
    gate_sem, up_sem, down_sem, gain_sem, x_sem, piece_sem, tile_sem, res_sem,
    peer_send, peer_recv, first_send, first_recv, mid_send, mid_recv, near_send, near_recv, far_send, far_recv,
    last_send, last_recv, whole_send, whole_recv, swap_send, swap_recv, load_sem,
):
    me = lax.axis_index("tp")
    chips = n // CORES
    chip, core = me // CORES, lax.rem(me, CORES)
    own_rows = residual.shape[0]
    half = own_rows // 2
    tiles = half // ROWS
    depth, width = w_gate.shape[1], w_down.shape[1]
    half_depth = depth // 2

    def device(c, k):
        return {"tp": lax.rem(c + chips, chips) * CORES + k}

    right, left, peer = device(chip + 1, core), device(chip - 1, core), device(chip, 1 - core)
    next_dev = (right, left)
    last = tiles - 1
    last_place = last % FAR_SLOTS

    def x_copies(stg, t, slot):
        (c0, h0), (c1, h1) = (
            ((chip + 2, 0), (chip + 2, 1)),
            ((chip + 2, 0), (chip + 2, 1)),
            ((chip + 1, 1), (chip - 1, 0)),
            ((chip + 1, 0), (chip - 1, 1)),
            ((chip, 0), (chip, 1)),
        )[stg]
        out = []
        for d, (c, h) in enumerate(((c0, h0), (c1, h1))):
            c = lax.rem(c + chips, chips)
            row = pl.multiple_of((c * CORES + core) * own_rows + h * half + t * ROWS, ROWS)
            out.append(pltpu.make_async_copy(
                x_in.at[pl.ds(row, ROWS)], x_tile.at[slot, pl.ds(d * ROWS, ROWS)], x_sem.at[slot, d]))
        return out

    def start_x(stg, t, slot):
        for cp in x_copies(stg, t, slot):
            cp.start()

    def wait_x(stg, t, slot):
        for cp in x_copies(stg, t, slot):
            cp.wait()

    def piece_copies(i):
        out = []
        for d in (RIGHT, LEFT):
            row = pl.multiple_of((lax.rem(chip + 2, chips) * CORES + core) * own_rows + d * half + i * FIRST, FIRST)
            out.append(pltpu.make_async_copy(
                x_in.at[pl.ds(row, FIRST)], x_tile.at[0, pl.ds((2 * i + d) * FIRST, FIRST)], piece_sem.at[i, d]))
        return out

    def own_cols(j):
        cols = pl.ds(pl.multiple_of(j * WCOLS, WCOLS), WCOLS)
        return [
            pltpu.make_async_copy(w_gate.at[:, cols], gate_w.at[core, :, cols], gate_sem.at[j]),
            pltpu.make_async_copy(w_up.at[:, cols], up_w.at[core, :, cols], up_sem.at[j]),
        ]

    def own_down(j):
        cols = pl.ds(pl.multiple_of(j * YCOLS, YCOLS), YCOLS)
        return pltpu.make_async_copy(w_down.at[:, cols], down_w.at[core, :, cols], down_sem.at[j])

    own_gain = pltpu.make_async_copy(norm_gain, gain, gain_sem)
    loads = [own_cols(j) for j in range(depth // WCOLS)] + [[own_down(j)] for j in range(width // YCOLS)]

    def start_load(i):
        for cp in loads[i] if i < len(loads) else ():
            cp.start()

    def wait_load(i):
        for cp in loads[i]:
            cp.wait()
        start_load(i + AHEAD)

    for cp in piece_copies(0):
        cp.start()
    for i in range(AHEAD):
        start_load(i)
    for k in range(1, ROWS // FIRST):
        for cp in piece_copies(k):
            cp.start()

    barrier = pltpu.get_barrier_semaphore()
    for dev in (peer, left, right):
        pl.semaphore_signal(barrier, inc=1, device_id=dev, device_id_type=pl.DeviceIdType.MESH)

    def remote(src, dst, send, recv, dev):
        return pltpu.make_async_remote_copy(
            src_ref=src, dst_ref=dst, send_sem=send, recv_sem=recv, device_id=dev, device_id_type=pl.DeviceIdType.MESH)

    peer_w = [
        remote(w, dst.at[core], peer_send.at[i], peer_recv.at[i], peer)
        for i, (w, dst) in enumerate(((w_gate, gate_w), (w_up, up_w), (w_down, down_w)))]
    my_half = pl.ds(pl.multiple_of(core * half_depth, half_depth), half_depth)

    def down_copy(d, src):
        return remote(src, down_in.at[d, my_half], whole_send.at[d], whole_recv.at[d], next_dev[d])

    def swap_copy(d):
        return remote(down_in.at[d, my_half], down_in.at[d, my_half], swap_send.at[d], swap_recv.at[d], peer)

    @pl.when(core == 0)
    def _():
        pl.semaphore_wait(barrier, 3)
        for d in (RIGHT, LEFT):
            down_copy(d, w_down.at[pl.ds(0, half_depth)]).start()

    def rows_of(t):
        return pl.ds(pl.multiple_of(t * ROWS, ROWS), ROWS)

    def mid_y(d, t):
        return remote(result.at[1, d, rows_of(t)], y_in.at[0, d, rows_of(t)], mid_send.at[1, d, t], mid_recv.at[1, d, t], next_dev[d])

    def mid_g(d, t):
        return remote(result.at[0, d, rows_of(t), pl.ds(0, depth)], g_in.at[0, d, rows_of(t)],
                      mid_send.at[0, d, t], mid_recv.at[0, d, t], next_dev[d])

    def near_copies(d, t, place):
        return [
            remote(near_g.at[place, d], g_in.at[1, d, rows_of(t)], near_send.at[place, d, 0], near_recv.at[0, d, t], next_dev[d]),
            remote(near_y.at[place, d], y_in.at[1, d, rows_of(t)], near_send.at[place, d, 1], near_recv.at[1, d, t], next_dev[d]),
        ]

    def far_copy(d, t, place):
        return remote(stage.at[place, d], far_in.at[d, rows_of(t)], far_send.at[place, d], far_recv.at[d, t], next_dev[d])

    def last_copy(d, i):
        here = pl.ds(last * ROWS + i * SUB, SUB)
        return remote(stage.at[last_place, d, pl.ds(i * SUB, SUB)], far_in.at[d, here],
                      last_send.at[d, i], last_recv.at[d, i], next_dev[d])

    def piece_copy(d, i, j):
        here, cols = pl.ds(i * FIRST, FIRST), pl.ds(j * YCOLS, YCOLS)
        return remote(result.at[1, d, here, cols], y_in.at[0, d, here, cols],
                      first_send.at[d, i, j], first_recv.at[d, i, j], next_dev[d])

    pieces = [(d, i, j) for i in range(ROWS // FIRST) for j in range(width // YCOLS) for d in (RIGHT, LEFT)]

    def make_hidden(slot, s, piece=None):
        rows = pl.ds(0, 2 * ROWS) if piece is None else pl.ds(piece * 2 * FIRST, 2 * FIRST)

        def chunk(j, _):
            if piece == 0:
                wait_load(j)
            cols = pl.ds(pl.multiple_of(j * WCOLS, WCOLS), WCOLS)
            x = x_tile[slot, rows]
            gate = jnp.dot(x, gate_w[s, :, cols], preferred_element_type=jnp.float32)
            up = jnp.dot(x, up_w[s, :, cols], preferred_element_type=jnp.float32)
            hidden[s, rows, cols] = (jax.nn.silu(gate) * up).astype(jnp.bfloat16)
            return 0
        if piece == 0:
            for j in range(depth // WCOLS):
                chunk(j, 0)
        else:
            lax.fori_loop(0, depth // WCOLS, chunk, 0)

    def part(s, cols, rows=pl.ds(0, 2 * ROWS)):
        return jnp.dot(hidden[s, rows], down_w[s, :, cols], preferred_element_type=jnp.float32).astype(jnp.bfloat16)

    def both(slot, store):
        make_hidden(slot, 0)
        make_hidden(slot, 1)

        def chunk(j, _):
            cols = pl.ds(pl.multiple_of(j * YCOLS, YCOLS), YCOLS)
            store(cols, part(0, cols).astype(jnp.float32) + part(1, cols).astype(jnp.float32))
            return 0
        lax.fori_loop(0, width // YCOLS, chunk, 0)

    def start_pieces():
        for piece in pieces:
            piece_copy(*piece).start()

    for i in range(ROWS // FIRST):
        rows = pl.ds(i * 2 * FIRST, 2 * FIRST)
        for cp in piece_copies(i):
            cp.wait()
        make_hidden(0, core, piece=i)

        @pl.when(core == 1)
        def _(i=i, rows=rows):
            if i == 0:
                pl.semaphore_wait(barrier, 3)
            for j in range(width // YCOLS):
                if i == 0:
                    wait_load(depth // WCOLS + j)
                cols = pl.ds(j * YCOLS, YCOLS)
                y = part(1, cols, rows)
                for d in (RIGHT, LEFT):
                    result[1, d, pl.ds(i * FIRST, FIRST), cols] = y[d * FIRST:(d + 1) * FIRST]
                for d in (RIGHT, LEFT):
                    piece_copy(d, i, j).start()

        @pl.when(core == 0)
        def _(i=i):
            for j in range(width // YCOLS) if i == 0 else ():
                wait_load(depth // WCOLS + j)
            for d in (RIGHT, LEFT):
                result[0, d, pl.ds(i * FIRST, FIRST), pl.ds(0, depth)] = hidden[0, pl.ds((2 * i + d) * FIRST, FIRST)]
        if i == 0:
            own_gain.start()
            for cp in peer_w:
                cp.start()
            start_x(0, 1, 1)

    @pl.when(core == 0)
    def _():
        for d in (RIGHT, LEFT):
            mid_g(d, 0).start()

    def mid_step(stg, t, s):
        slot = lax.rem(t, 2)

        @pl.when(t < last)
        def _():
            start_x(stg, t + 1, 1 - slot)

        @pl.when(t == last)
        def _():
            start_x(stg + 1, 0, 1 - slot)
        wait_x(stg, t, slot)
        make_hidden(slot, s)

        @pl.when(s == 0)
        def _():
            for d in (RIGHT, LEFT):
                result[0, d, rows_of(t), pl.ds(0, depth)] = hidden[0, pl.ds(d * ROWS, ROWS)]
            for d in (RIGHT, LEFT):
                mid_g(d, t).start()

        @pl.when(s == 1)
        def _():
            def chunk(j, _):
                cols = pl.ds(pl.multiple_of(j * YCOLS, YCOLS), YCOLS)
                y = part(1, cols)
                for d in (RIGHT, LEFT):
                    result[1, d, rows_of(t), cols] = y[d * ROWS:(d + 1) * ROWS]
                return 0
            lax.fori_loop(0, width // YCOLS, chunk, 0)

            @pl.when(t == 0)
            def _():
                start_pieces()

            @pl.when(t > 0)
            def _():
                for d in (RIGHT, LEFT):
                    mid_y(d, t).start()

    def loop(t0, t1, step):
        def body(t, _):
            step(t)
            return 0
        lax.fori_loop(t0, t1, body, 0)

    loop(1, tiles, lambda t: mid_step(0, t, core))
    for cp in peer_w:
        cp.wait_recv()

    @pl.when(core == 1)
    def _():
        for d in (RIGHT, LEFT):
            down_copy(d, down_w.at[0, pl.ds(half_depth, half_depth)]).start()
    loop(0, tiles, lambda t: mid_step(1, t, 1 - core))

    def near_step(t):
        slot, place = lax.rem(t, 2), lax.rem(t, NEAR_SLOTS)

        for now, stg, nxt in ((0, 2, 1), (NEAR_SLOTS - 1, 4, 0), (NEAR_SLOTS, 2, NEAR_SLOTS + 1), (last, 3, 0)):
            @pl.when(t == now)
            def _(stg=stg, nxt=nxt):
                start_x(stg, nxt, 1 - slot)
        wait_x(2, t, slot)
        make_hidden(slot, 0)
        make_hidden(slot, 1)

        @pl.when(t >= NEAR_SLOTS)
        def _():
            for d in (RIGHT, LEFT):
                for cp in near_copies(d, t - NEAR_SLOTS, place):
                    cp.wait_send()
        for d in (RIGHT, LEFT):
            near_g[place, d] = hidden[0, pl.ds(d * ROWS, ROWS)]

        def chunk(j, _):
            cols = pl.ds(pl.multiple_of(j * YCOLS, YCOLS), YCOLS)
            y = part(1, cols)
            for d in (RIGHT, LEFT):
                near_y[place, d, :, cols] = y[d * ROWS:(d + 1) * ROWS]
            return 0
        lax.fori_loop(0, width // YCOLS, chunk, 0)
        for d in (RIGHT, LEFT):
            for cp in near_copies(d, t, place):
                cp.start()
    loop(0, NEAR_SLOTS, near_step)

    def own_step(t):
        slot = lax.rem(t, 2)

        @pl.when(t < last)
        def _():
            start_x(4, t + 1, 1 - slot)

        @pl.when(t == last)
        def _():
            start_x(2, NEAR_SLOTS, 1 - slot)
        wait_x(4, t, slot)
        res_copies = [pltpu.make_async_copy(
            residual.at[pl.ds(pl.multiple_of(h * half + t * ROWS, ROWS), ROWS)], y_tile.at[h], res_sem.at[h]) for h in (0, 1)]
        for cp in res_copies:
            cp.start()
        for cp in res_copies:
            cp.wait()

        def store(cols, y):
            for h in (0, 1):
                acc[h, rows_of(t), cols] = y[h * ROWS:(h + 1) * ROWS] + y_tile[h, :, cols].astype(jnp.float32)
        both(slot, store)

    loop(0, tiles, own_step)

    for d in (RIGHT, LEFT):
        down_copy(d, w_down.at[pl.ds(0, half_depth)]).wait_recv()
        swap_copy(d).start()
    for piece in pieces:
        piece_copy(*piece).wait_send()
    loop(0, tiles, lambda t: [mid_g(d, t).wait_send() for d in (RIGHT, LEFT)])
    loop(1, tiles, lambda t: [mid_y(d, t).wait_send() for d in (RIGHT, LEFT)])
    for d in (RIGHT, LEFT):
        swap_copy(d).wait_recv()
    loads = [pltpu.make_async_copy(down_in.at[d, pl.ds(h * half_depth, half_depth)], result.at[d, h], load_sem.at[d, h])
             for d in (RIGHT, LEFT) for h in (0, 1)]
    for cp in loads:
        cp.start()
    for cp in loads:
        cp.wait()

    loop(NEAR_SLOTS, tiles, near_step)


    def load_terms(kind, t):
        cps = []
        for d in (RIGHT, LEFT):
            cps.append(pltpu.make_async_copy(y_in.at[kind, d, rows_of(t)], y_tile.at[d], tile_sem.at[1, d]))
            cps.append(pltpu.make_async_copy(g_in.at[kind, d, rows_of(t)], g_tile.at[d], tile_sem.at[0, d]))
        return cps

    def term(d, cols):
        w = result[d, :, :, cols].reshape(depth, YCOLS)
        y = jnp.dot(g_tile[d], w, preferred_element_type=jnp.float32).astype(jnp.bfloat16)
        return y.astype(jnp.float32) + y_tile[d, :, cols].astype(jnp.float32)

    def far_tile(t, slot, place):
        wait_x(3, t, slot)

        def store(cols, y):
            for d in (RIGHT, LEFT):
                stage[place, d, :, cols] = y[d * ROWS:(d + 1) * ROWS]
        both(slot, store)
        for d in (RIGHT, LEFT):
            mid_g(d, t).wait_recv()

        @pl.when(t == 0)
        def _():
            for piece in pieces:
                piece_copy(*piece).wait_recv()

        @pl.when(t > 0)
        def _():
            for d in (RIGHT, LEFT):
                mid_y(d, t).wait_recv()
        for cp in load_terms(0, t):
            cp.start()
        for cp in load_terms(0, t):
            cp.wait()

        def chunk(j, _):
            cols = pl.ds(pl.multiple_of(j * YCOLS, YCOLS), YCOLS)
            for d in (RIGHT, LEFT):
                stage[place, d, :, cols] += term(d, cols)
            return 0
        lax.fori_loop(0, width // YCOLS, chunk, 0)

    def far_step(t):
        slot, place = lax.rem(t, 2), lax.rem(t, FAR_SLOTS)

        @pl.when(t < last)
        def _():
            start_x(3, t + 1, 1 - slot)

        @pl.when(t >= FAR_SLOTS)
        def _():
            for d in (RIGHT, LEFT):
                far_copy(d, t - FAR_SLOTS, place).wait_send()
        far_tile(t, slot, place)

        @pl.when(t < last)
        def _():
            for d in (RIGHT, LEFT):
                far_copy(d, t, place).start()

        @pl.when(t == last)
        def _():
            for i in range(ROWS // SUB):
                for d in (RIGHT, LEFT):
                    last_copy(d, i).start()
    loop(0, tiles, far_step)

    def own_terms(t):
        for d in (RIGHT, LEFT):
            for cp in near_copies(d, t, 0):
                cp.wait_recv()
        for cp in load_terms(1, t):
            cp.start()
        for cp in load_terms(1, t):
            cp.wait()

        def chunk(j, _):
            cols = pl.ds(pl.multiple_of(j * YCOLS, YCOLS), YCOLS)
            for h in (0, 1):
                acc[h, rows_of(t), cols] += term(1 - h, cols)
            return 0
        lax.fori_loop(0, width // YCOLS, chunk, 0)

    loop(0, tiles, own_terms)

    for cp in peer_w:
        cp.wait_send()
    for d in (RIGHT, LEFT):
        down_copy(d, w_down.at[pl.ds(0, half_depth)]).wait_send()
        swap_copy(d).wait_send()
        for place in range(NEAR_SLOTS):
            for cp in near_copies(d, 0, place):
                cp.wait_send()
    own_gain.wait()

    def finish(row):
        for h in (0, 1):
            here = pl.ds(row, 16)
            value = acc[h, here] + far_in[h, here]
            mean_sq = jnp.mean(value * value, axis=-1, keepdims=True)
            result[0, h, here] = value.astype(jnp.bfloat16)
            result[1, h, here] = (value * lax.rsqrt(mean_sq + EPS) * gain[...]).astype(jnp.bfloat16)

    def last_step(t):
        for d in (RIGHT, LEFT):
            far_copy(d, t, 0).wait_recv()
        loop(0, ROWS // 16, lambda j: finish(pl.multiple_of(t * ROWS + j * 16, 16)))
    loop(0, last, last_step)

    for place in range(FAR_SLOTS):
        if place != last_place:
            for d in (RIGHT, LEFT):
                far_copy(d, 0, place).wait_send()

    for i in range(ROWS // SUB):
        for d in (RIGHT, LEFT):
            last_copy(d, i).wait_recv()
        for j in range(SUB // 16):
            finish(last * ROWS + i * SUB + j * 16)
    for i in range(ROWS // SUB):
        for d in (RIGHT, LEFT):
            last_copy(d, i).wait_send()


def write_kernel(result, h_out, normed, sem):
    half = result.shape[2]
    copies = [
        pltpu.make_async_copy(result.at[i, h], out.at[pl.ds(h * half, half)], sem.at[i, h])
        for i, out in enumerate((h_out, normed)) for h in (0, 1)]
    for cp in copies:
        cp.start()
    for cp in copies:
        cp.wait()


def solution(mesh):
    n = mesh.shape["tp"]

    def local_block(x_in, w_gate, w_up, w_down, residual, norm_gain):
        rows, width = residual.shape
        depth = w_gate.shape[1]
        half = rows // 2
        tiles = half // ROWS
        f32, bf16 = jnp.float32, jnp.bfloat16
        dma = pltpu.SemaphoreType.DMA
        any_space = pl.BlockSpec(memory_space=pl.ANY)
        result, _, _, _ = pl.pallas_call(
            functools.partial(ring_kernel, n),
            out_shape=(
                pltpu.VMEM((2, 2, half, width), bf16),
                jax.ShapeDtypeStruct((2, 2, half, width), bf16),
                jax.ShapeDtypeStruct((2, 2, half, depth), bf16),
                jax.ShapeDtypeStruct((2, depth, width), bf16),
            ),
            in_specs=[any_space] * 6,
            out_specs=(pl.BlockSpec(memory_space=pltpu.VMEM),) + (any_space,) * 3,
            scratch_shapes=[
                pltpu.VMEM((2,) + w_gate.shape, bf16),
                pltpu.VMEM((2,) + w_up.shape, bf16),
                pltpu.VMEM((2,) + w_down.shape, bf16),
                pltpu.VMEM((2, 2 * ROWS, width), bf16),
                pltpu.VMEM((2, 2 * ROWS, depth), bf16),
                pltpu.VMEM((NEAR_SLOTS, 2, ROWS, width), bf16),
                pltpu.VMEM((NEAR_SLOTS, 2, ROWS, depth), bf16),
                pltpu.VMEM((FAR_SLOTS, 2, ROWS, width), f32),
                pltpu.VMEM((2, half, width), f32),
                pltpu.VMEM((2, half, width), f32),
                pltpu.VMEM((2, ROWS, width), bf16),
                pltpu.VMEM((2, ROWS, depth), bf16),
                pltpu.VMEM((1, width), f32),
                dma((depth // WCOLS,)), dma((depth // WCOLS,)), dma((width // YCOLS,)), dma(()), dma((2, 2)),
                dma((ROWS // FIRST, 2)), dma((2, 2)), dma((2,)),
                dma((3,)), dma((3,)),
                dma((2, ROWS // FIRST, width // YCOLS)), dma((2, ROWS // FIRST, width // YCOLS)),
                dma((2, 2, tiles)), dma((2, 2, tiles)),
                dma((NEAR_SLOTS, 2, 2)), dma((2, 2, tiles)),
                dma((FAR_SLOTS, 2)), dma((2, tiles)),
                dma((2, ROWS // SUB)), dma((2, ROWS // SUB)),
                dma((2,)), dma((2,)), dma((2,)), dma((2,)), dma((2, 2)),
            ],
            compiler_params=pltpu.CompilerParams(
                collective_id=0, has_side_effects=True, vmem_limit_bytes=VMEM_LIMIT),
            name="ring",
        )(x_in, w_gate, w_up, w_down, residual, norm_gain.reshape(1, width))
        return pl.pallas_call(
            write_kernel,
            out_shape=(jax.ShapeDtypeStruct((rows, width), bf16),) * 2,
            in_specs=[pl.BlockSpec(memory_space=pltpu.VMEM)],
            out_specs=(any_space, any_space),
            scratch_shapes=[dma((2, 2))],
            compiler_params=pltpu.CompilerParams(vmem_limit_bytes=2**20),
            name="write",
        )(pltpu.with_memory_space_constraint(result, pltpu.VMEM))

    row_spec = P(("data", "tp"), None)
    return jax.shard_map(local_block, mesh=mesh, in_specs=(P("data", None), P(None, "tp"), P(None, "tp"), P("tp", None), row_spec, P(None)), out_specs=(row_spec, row_spec), check_vma=False)
```

time: 285 us -> 282 us (0.989)
  Pallas kernels: 284 us -> 279 us
    pallas_call x1, Pallas kernels: 280 us -> 276 us  [local_block(): pl.pallas_call(functools.partial(ring_kernel, n), out_shape=(pltpu.VMEM((...]
where the time goes in v4:
time: 282 us; the launch traced here: 280 us
  Pallas kernels  279 us (99%)
    pallas_call x1, Pallas kernels, local_block(): pl.pallas_call(functools.partial(ring_kernel, n), out_shape=(pltpu.VMEM((...  276 us

profile of v4, /device:TPU:112, one launch (start us, length us, event | category | flops | bytes accessed | tf_op | source)
XLA Modules:
  0.0 280.2 jit_solution(4681090243833603138)
XLA Ops:
  0.6 276.0 %ring.1 = (bf16[2,2,512,2048]{3,2,1,0:T(8,128)(2,1)S(1)}, bf16[2,2,512,2048]{3,2,1,0:T(8,128)(2,1)}, bf16[2,2,512,1024]{3,2,1,0:T(8,128)(2,1)}, bf16[2,1024,2048]{2,1,0:T(8,128)(2,1)}) custom-call(bf16[8192,2048]{1,0:T(8,128)(2,1)} %x_in.1, bf16[2048,1024]{1,0:T(8,128)(2,1)} %w_gate.1, bf16[2048,1024]{1,0:T(8,128)(2,1)} %w_up.1, bf16[1024,2048]{1,0:T(8,128)(2,1)} %w_down.1, ...), custom_call_target="tpu_custom_call" | custom-call | tf_op jit(solution)/shard_map/ring/pallas_call | solution.py:515
  276.6 3.4 %write.1 = (bf16[1024,2048]{1,0:T(8,128)(2,1)}, bf16[1024,2048]{1,0:T(8,128)(2,1)}) custom-call(bf16[2,2,512,2048]{3,2,1,0:T(8,128)(2,1)S(1)} %get-tuple-element.3.result), custom_call_target="tpu_custom_call" | custom-call | tf_op jit(solution)/shard_map/write/pallas_call | solution.py:553

commit v5 on v4

--- a/solution.py
+++ b/solution.py
@@ -29,20 +29,48 @@
 ):
     me = lax.axis_index("tp")
     chips = n // CORES
-    chip, core = me // CORES, lax.rem(me, CORES)
+    chip, core = me // CORES, CORES - 1 - lax.rem(me, CORES)
     own_rows = residual.shape[0]
     half = own_rows // 2
     tiles = half // ROWS
     depth, width = w_gate.shape[1], w_down.shape[1]
     half_depth = depth // 2
 
+    def position(c, k):
+        return lax.rem(c + chips, chips) * CORES + CORES - 1 - k
+
     def device(c, k):
-        return {"tp": lax.rem(c + chips, chips) * CORES + k}
+        return {"tp": position(c, k)}
 
     right, left, peer = device(chip + 1, core), device(chip - 1, core), device(chip, 1 - core)
     next_dev = (right, left)
     last = tiles - 1
     last_place = last % FAR_SLOTS
+
+    barrier = pltpu.get_barrier_semaphore()
+    for dev in (peer, left, right):
+        pl.semaphore_signal(barrier, inc=1, device_id=dev, device_id_type=pl.DeviceIdType.MESH)
+
+    def remote(src, dst, send, recv, dev):
+        return pltpu.make_async_remote_copy(
+            src_ref=src, dst_ref=dst, send_sem=send, recv_sem=recv, device_id=dev, device_id_type=pl.DeviceIdType.MESH)
+
+    peer_w = [
+        remote(w, dst.at[core], peer_send.at[i], peer_recv.at[i], peer)
+        for i, (w, dst) in enumerate(((w_gate, gate_w), (w_up, up_w), (w_down, down_w)))]
+    my_half = pl.ds(pl.multiple_of(core * half_depth, half_depth), half_depth)
+
+    def down_copy(d, src):
+        return remote(src, down_in.at[d, my_half], whole_send.at[d], whole_recv.at[d], next_dev[d])
+
+    def swap_copy(d):
+        return remote(down_in.at[d, my_half], down_in.at[d, my_half], swap_send.at[d], swap_recv.at[d], peer)
+
+    @pl.when(core == 0)
+    def _():
+        pl.semaphore_wait(barrier, 3)
+        for d in (RIGHT, LEFT):
+            down_copy(d, w_down.at[pl.ds(0, half_depth)]).start()
 
     def x_copies(stg, t, slot):
         (c0, h0), (c1, h1) = (
@@ -54,8 +82,7 @@
         )[stg]
         out = []
         for d, (c, h) in enumerate(((c0, h0), (c1, h1))):
-            c = lax.rem(c + chips, chips)
-            row = pl.multiple_of((c * CORES + core) * own_rows + h * half + t * ROWS, ROWS)
+            row = pl.multiple_of(position(c, core) * own_rows + h * half + t * ROWS, ROWS)
             out.append(pltpu.make_async_copy(
                 x_in.at[pl.ds(row, ROWS)], x_tile.at[slot, pl.ds(d * ROWS, ROWS)], x_sem.at[slot, d]))
         return out
@@ -71,7 +98,7 @@
     def piece_copies(i):
         out = []
         for d in (RIGHT, LEFT):
-            row = pl.multiple_of((lax.rem(chip + 2, chips) * CORES + core) * own_rows + d * half + i * FIRST, FIRST)
+            row = pl.multiple_of(position(chip + 2, core) * own_rows + d * half + i * FIRST, FIRST)
             out.append(pltpu.make_async_copy(
                 x_in.at[pl.ds(row, FIRST)], x_tile.at[0, pl.ds((2 * i + d) * FIRST, FIRST)], piece_sem.at[i, d]))
         return out
@@ -106,31 +133,6 @@
     for k in range(1, ROWS // FIRST):
         for cp in piece_copies(k):
             cp.start()
-
-    barrier = pltpu.get_barrier_semaphore()
-    for dev in (peer, left, right):
-        pl.semaphore_signal(barrier, inc=1, device_id=dev, device_id_type=pl.DeviceIdType.MESH)
-
-    def remote(src, dst, send, recv, dev):
-        return pltpu.make_async_remote_copy(
-            src_ref=src, dst_ref=dst, send_sem=send, recv_sem=recv, device_id=dev, device_id_type=pl.DeviceIdType.MESH)
-
-    peer_w = [
-        remote(w, dst.at[core], peer_send.at[i], peer_recv.at[i], peer)
-        for i, (w, dst) in enumerate(((w_gate, gate_w), (w_up, up_w), (w_down, down_w)))]
-    my_half = pl.ds(pl.multiple_of(core * half_depth, half_depth), half_depth)
-
-    def down_copy(d, src):
-        return remote(src, down_in.at[d, my_half], whole_send.at[d], whole_recv.at[d], next_dev[d])
-
-    def swap_copy(d):
-        return remote(down_in.at[d, my_half], down_in.at[d, my_half], swap_send.at[d], swap_recv.at[d], peer)
-
-    @pl.when(core == 0)
-    def _():
-        pl.semaphore_wait(barrier, 3)
-        for d in (RIGHT, LEFT):
-            down_copy(d, w_down.at[pl.ds(0, half_depth)]).start()
 
     def rows_of(t):
         return pl.ds(pl.multiple_of(t * ROWS, ROWS), ROWS)

time: 282 us -> 281 us (level)
  no operation moved by 1% of the time
where the time goes in v5:
time: 281 us
  Pallas kernels  280 us (100%)
    pallas_call x1, Pallas kernels, local_block(): pl.pallas_call(functools.partial(ring_kernel, n), out_shape=(pltpu.VMEM((...  277 us

profile of v5, /device:TPU:112, one launch (start us, length us, event | category | flops | bytes accessed | tf_op | source)
XLA Modules:
  0.0 280.7 jit_solution(10674138126091659245)
XLA Ops:
  0.6 276.6 %ring.1 = (bf16[2,2,512,2048]{3,2,1,0:T(8,128)(2,1)S(1)}, bf16[2,2,512,2048]{3,2,1,0:T(8,128)(2,1)}, bf16[2,2,512,1024]{3,2,1,0:T(8,128)(2,1)}, bf16[2,1024,2048]{2,1,0:T(8,128)(2,1)}) custom-call(bf16[8192,2048]{1,0:T(8,128)(2,1)} %x_in.1, bf16[2048,1024]{1,0:T(8,128)(2,1)} %w_gate.1, bf16[2048,1024]{1,0:T(8,128)(2,1)} %w_up.1, bf16[1024,2048]{1,0:T(8,128)(2,1)} %w_down.1, ...), custom_call_target="tpu_custom_call" | custom-call | tf_op jit(solution)/shard_map/ring/pallas_call | solution.py:517
  277.2 3.4 %write.1 = (bf16[1024,2048]{1,0:T(8,128)(2,1)}, bf16[1024,2048]{1,0:T(8,128)(2,1)}) custom-call(bf16[2,2,512,2048]{3,2,1,0:T(8,128)(2,1)S(1)} %get-tuple-element.3.result), custom_call_target="tpu_custom_call" | custom-call | tf_op jit(solution)/shard_map/write/pallas_call | solution.py:555

commit v6 on v5

--- a/solution.py
+++ b/solution.py
@@ -25,7 +25,7 @@
     gate_w, up_w, down_w, x_tile, hidden, near_y, near_g, stage, far_in, acc, y_tile, g_tile, gain,
     gate_sem, up_sem, down_sem, gain_sem, x_sem, piece_sem, tile_sem, res_sem,
     peer_send, peer_recv, first_send, first_recv, mid_send, mid_recv, near_send, near_recv, far_send, far_recv,
-    last_send, last_recv, whole_send, whole_recv, swap_send, swap_recv, load_sem,
+    last_send, last_recv, whole_send, whole_recv, swap_send, swap_recv, load_sem, partner_in,
 ):
     me = lax.axis_index("tp")
     chips = n // CORES
@@ -48,8 +48,16 @@
     last_place = last % FAR_SLOTS
 
     barrier = pltpu.get_barrier_semaphore()
-    for dev in (peer, left, right):
-        pl.semaphore_signal(barrier, inc=1, device_id=dev, device_id_type=pl.DeviceIdType.MESH)
+
+    def greet(dev, sem=barrier):
+        pl.semaphore_signal(sem, inc=1, device_id=dev, device_id_type=pl.DeviceIdType.MESH)
+
+    for dev in (left, right):
+        greet(dev)
+
+    @pl.when(core == 0)
+    def _():
+        greet(peer)
 
     def remote(src, dst, send, recv, dev):
         return pltpu.make_async_remote_copy(
@@ -68,7 +76,7 @@
 
     @pl.when(core == 0)
     def _():
-        pl.semaphore_wait(barrier, 3)
+        pl.semaphore_wait(barrier, 2)
         for d in (RIGHT, LEFT):
             down_copy(d, w_down.at[pl.ds(0, half_depth)]).start()
 
@@ -210,6 +218,7 @@
         def _(i=i, rows=rows):
             if i == 0:
                 pl.semaphore_wait(barrier, 3)
+                greet(peer, partner_in)
             for j in range(width // YCOLS):
                 if i == 0:
                     wait_load(depth // WCOLS + j)
@@ -228,6 +237,10 @@
                 result[0, d, pl.ds(i * FIRST, FIRST), pl.ds(0, depth)] = hidden[0, pl.ds((2 * i + d) * FIRST, FIRST)]
         if i == 0:
             own_gain.start()
+
+            @pl.when(core == 0)
+            def _():
+                pl.semaphore_wait(partner_in, 1)
             for cp in peer_w:
                 cp.start()
             start_x(0, 1, 1)
@@ -546,7 +559,7 @@
                 dma((NEAR_SLOTS, 2, 2)), dma((2, 2, tiles)),
                 dma((FAR_SLOTS, 2)), dma((2, tiles)),
                 dma((2, ROWS // SUB)), dma((2, ROWS // SUB)),
-                dma((2,)), dma((2,)), dma((2,)), dma((2,)), dma((2, 2)),
+                dma((2,)), dma((2,)), dma((2,)), dma((2,)), dma((2, 2)), pltpu.SemaphoreType.REGULAR,
             ],
             compiler_params=pltpu.CompilerParams(
                 collective_id=0, has_side_effects=True, vmem_limit_bytes=VMEM_LIMIT),

time: 281 us -> 281 us (level)
  no operation moved by 1% of the time
where the time goes in v6:
time: 281 us
  Pallas kernels  280 us (100%)
    pallas_call x1, Pallas kernels, local_block(): pl.pallas_call(functools.partial(ring_kernel, n), out_shape=(pltpu.VMEM((...  276 us

profile of v6, /device:TPU:112, one launch (start us, length us, event | category | flops | bytes accessed | tf_op | source)
XLA Modules:
  0.0 280.6 jit_solution(17683422281948980099)
XLA Ops:
  0.6 276.4 %ring.1 = (bf16[2,2,512,2048]{3,2,1,0:T(8,128)(2,1)S(1)}, bf16[2,2,512,2048]{3,2,1,0:T(8,128)(2,1)}, bf16[2,2,512,1024]{3,2,1,0:T(8,128)(2,1)}, bf16[2,1024,2048]{2,1,0:T(8,128)(2,1)}) custom-call(bf16[8192,2048]{1,0:T(8,128)(2,1)} %x_in.1, bf16[2048,1024]{1,0:T(8,128)(2,1)} %w_gate.1, bf16[2048,1024]{1,0:T(8,128)(2,1)} %w_up.1, bf16[1024,2048]{1,0:T(8,128)(2,1)} %w_down.1, ...), custom_call_target="tpu_custom_call" | custom-call | tf_op jit(solution)/shard_map/ring/pallas_call | solution.py:530
  277.0 3.4 %write.1 = (bf16[1024,2048]{1,0:T(8,128)(2,1)}, bf16[1024,2048]{1,0:T(8,128)(2,1)}) custom-call(bf16[2,2,512,2048]{3,2,1,0:T(8,128)(2,1)S(1)} %get-tuple-element.3.result), custom_call_target="tpu_custom_call" | custom-call | tf_op jit(solution)/shard_map/write/pallas_call | solution.py:568

commit v7 on v6

--- a/solution.py
+++ b/solution.py
@@ -15,7 +15,7 @@
 FIRST = 64
 WCOLS = 256
 YCOLS = 512
-AHEAD = 4
+AHEAD = 8
 RIGHT, LEFT = 0, 1
 VMEM_LIMIT = 58_500_000
 

time: 281 us -> 281 us (level)
  no operation moved by 1% of the time
where the time goes in v7:
time: 281 us
  Pallas kernels  280 us (100%)
    pallas_call x1, Pallas kernels, local_block(): pl.pallas_call(functools.partial(ring_kernel, n), out_shape=(pltpu.VMEM((...  276 us

profile of v7, /device:TPU:112, one launch (start us, length us, event | category | flops | bytes accessed | tf_op | source)
XLA Modules:
  0.0 280.6 jit_solution(7271450248365365908)
XLA Ops:
  0.6 276.4 %ring.1 = (bf16[2,2,512,2048]{3,2,1,0:T(8,128)(2,1)S(1)}, bf16[2,2,512,2048]{3,2,1,0:T(8,128)(2,1)}, bf16[2,2,512,1024]{3,2,1,0:T(8,128)(2,1)}, bf16[2,1024,2048]{2,1,0:T(8,128)(2,1)}) custom-call(bf16[8192,2048]{1,0:T(8,128)(2,1)} %x_in.1, bf16[2048,1024]{1,0:T(8,128)(2,1)} %w_gate.1, bf16[2048,1024]{1,0:T(8,128)(2,1)} %w_up.1, bf16[1024,2048]{1,0:T(8,128)(2,1)} %w_down.1, ...), custom_call_target="tpu_custom_call" | custom-call | tf_op jit(solution)/shard_map/ring/pallas_call | solution.py:530
  277.0 3.4 %write.1 = (bf16[1024,2048]{1,0:T(8,128)(2,1)}, bf16[1024,2048]{1,0:T(8,128)(2,1)}) custom-call(bf16[2,2,512,2048]{3,2,1,0:T(8,128)(2,1)S(1)} %get-tuple-element.3.result), custom_call_target="tpu_custom_call" | custom-call | tf_op jit(solution)/shard_map/write/pallas_call | solution.py:568
